TPU v7x, 32 devices: a whole 2x2x4 slice. The times are simulated.
32 devices in a mesh: row: 8 (over z, y), ma: 4 (over x, core).
Axes of the slice: x: 2, y: 2, z: 4, core: 2. Of those that a mesh axis runs over, the one named last changes fastest.
Arguments:
- thermal_state: float32 [64, 768, 2048], P('row', None, 'ma'), may hold values from -6 to 6
- sphere_node_annulus: int32 [64, 768], P('row'), may hold values from 0 to 1022, as said below
- sphere_node_offset: float32 [64, 768], P('row'), may hold values from 0 to 1
- integration_share: float32 [64, 768], P('row'), may hold values from 0.02 to 0.2
- annulus_holder_row: int32 [1024], replicated, may hold values from 0 to 7, never falling along the last dimension, each value on 1 to 256 neighbouring positions
- rotating_flow_potential: float32 [2048, 2048], P('row', 'ma'), may hold values from -6 to 6
Outputs:
- thermal_state_later: float32 [64, 768, 2048], P('row', None, 'ma')
- flow_potential_later: float32 [2048, 2048], P('row', 'ma')
Inputs may be any that keep to these rules, and one draw needn't show every extreme that they name: `sphere_node_annulus`: lower cell of each point; the next cell exists. `annulus_holder_row`: never falling along cells; each owner holds 1 to 256 cells and some owner exactly 256.
All inputs are finite; a program needn't handle non-finite values.
Results may differ from a plain program's by a relative error of at most 0.0003.
Values sent between devices are 32-bit elements; how exact they have to be, the bound alone decides.
A program may use at most 64 MiB of HBM per device.

v0:
```python
import math

import jax
import jax.numpy as jnp
from jax import lax
from jax.sharding import PartitionSpec as P

stream_step = 0.5
thermal_advance = 0.25


def extended(x, sides, width, wrap):
    for axis, dim in sides:
        size, length = (lax.axis_size(axis), x.shape[dim])
        up = [(i, (i + 1) % size) for i in range(size if wrap else size - 1)]
        down = [(j, i) for i, j in up]
        last = lax.slice_in_dim(x, length - width, length, axis=dim)
        leading = lax.slice_in_dim(x, 0, width, axis=dim)
        before = lax.ppermute(last, axis, up)
        after = lax.ppermute(leading, axis, down)
        x = jnp.concatenate([before, x, after], axis=dim)
    return x


def phi_diff(field):
    return (field[:, 2:] - field[:, :-2]) * 0.5


def qg_step(zint, stream, geo_slots):
    geo_column = geo_slots[:, None]
    extended_field = extended(jnp.stack([zint, stream]), (("ma", 2),), 2, True)
    forcing = -geo_column * phi_diff(extended_field[0])
    stream_wide = extended_field[1][:, 1:-1] + stream_step * forcing
    velocity = geo_column * phi_diff(stream_wide)
    return (stream_wide[:, 1:-1], velocity)


def per_device(
    thermal_state,
    sphere_node_annulus,
    sphere_node_offset,
    integration_share,
    annulus_holder_row,
    rotating_flow_potential,
):
    sphere_level_list, meridian_total, longitude_total = thermal_state.shape
    slot_most = rotating_flow_potential.shape[0]
    cell_count = annulus_holder_row.shape[0]
    cells = jnp.arange(cell_count, dtype=jnp.int32)
    before = jnp.sum(
        (annulus_holder_row[None, :] < annulus_holder_row[:, None]).astype(jnp.int32), axis=1
    )
    slot_of_cell = annulus_holder_row * slot_most + cells - before
    geo_cell = 1.0 / (0.25 + (cells.astype(jnp.float32) + 0.5) / cell_count)
    lower_cell = sphere_node_annulus.reshape(-1)
    slot_low = slot_of_cell[lower_cell]
    slot_high = slot_of_cell[lower_cell + 1]
    fraction = sphere_node_offset.reshape(-1)
    quadrature = integration_share.reshape(-1)
    below_share = quadrature * (1.0 - fraction)
    above_share = quadrature * fraction
    heat_vector_linear = thermal_state.reshape(-1, longitude_total)
    own_index = lax.axis_index("row")
    own_start = own_index * slot_most
    slot_rows = jnp.arange(lax.axis_size("row") * slot_most, dtype=jnp.int32)
    banded = jnp.where(slot_rows[:, None] == slot_low[None, :], below_share[None, :], 0.0)
    banded = banded + jnp.where(slot_rows[:, None] == slot_high[None, :], above_share[None, :], 0.0)
    zint = lax.psum_scatter(
        jnp.dot(
            banded,
            heat_vector_linear,
            precision=lax.Precision.HIGHEST,
            preferred_element_type=jnp.float32,
        ),
        "row",
        scatter_dimension=0,
        tiled=True,
    )
    slot_rows = own_start + jnp.arange(slot_most, dtype=jnp.int32)
    hits = slot_of_cell[None, :] == slot_rows[:, None]
    flow_potential_later, velocity = qg_step(
        zint, rotating_flow_potential, jnp.sum(jnp.where(hits, geo_cell[None, :], 0.0), axis=1)
    )
    piece = lax.all_gather(velocity, "row", axis=0, tiled=True)
    slot_cols = jnp.arange(piece.shape[0], dtype=jnp.int32)
    interp = jnp.where(slot_low[:, None] == slot_cols[None, :], (1.0 - fraction)[:, None], 0.0)
    interp = interp + jnp.where(slot_high[:, None] == slot_cols[None, :], fraction[:, None], 0.0)
    shifted_heat = jnp.dot(
        interp, piece, precision=lax.Precision.HIGHEST, preferred_element_type=jnp.float32
    )
    sphere_node_drift = shifted_heat.reshape(sphere_level_list, meridian_total, longitude_total)
    annulus_edges = extended(thermal_state, (("row", 0),), 1, False)
    distance_from_centre = (annulus_edges[2:] - annulus_edges[:-2]) * 0.5
    wrapped_heat_grid = jnp.pad(thermal_state, ((0, 0), (1, 1), (0, 0)))
    theta_from_north = (wrapped_heat_grid[:, 2:] - wrapped_heat_grid[:, :-2]) * 0.5
    angle = math.pi * (jnp.arange(meridian_total, dtype=jnp.float32) + 0.5) / meridian_total
    sin_theta_term = jnp.sin(angle)[None, :, None]
    cos_theta_term = jnp.cos(angle)[None, :, None]
    thermal_state_later = thermal_state - thermal_advance * sphere_node_drift * (
        sin_theta_term * distance_from_centre + cos_theta_term * theta_from_north
    )
    return (thermal_state_later, flow_potential_later)


def solution(mesh):
    return jax.shard_map(
        per_device,
        mesh=mesh,
        in_specs=(
            P("row", None, "ma"),
            P("row", None),
            P("row", None),
            P("row", None),
            P(),
            P("row", "ma"),
        ),
        out_specs=(P("row", None, "ma"), P("row", "ma")),
        check_vma=False,
    )
```

profile of v0, /device:TPU:0, one launch (start us, length us, event | category | flops | bytes accessed | tf_op | source)
XLA Modules:
  0.0 537.9 jit_solution(14528305836900812789)
XLA Ops:
  7.2 0.0 reduce-scatter.2.cloned.1.call-start
  7.2 1.3 convert_reduce_fusion
  8.5 0.7 add_subtract_fusion
  9.2 0.7 reshape.131
  10.0 0.8 copy.8
  10.7 0.7 reshape.132
  11.5 0.1 compare_select_fusion.1
  11.6 24.8 %gather_fusion = s32[6144]{0:T(1024)S(1)} fusion(s32[1024]{0:T(1024)S(1)} %add_subtract_fusion, s32[6144]{0:T(1024)S(1)} %broadcast_clamp_fusion.1), kind=kCustom, calls=%fused_computation | custom fusion | bytes 73728 | tf_op jit(solution)/shard_map/gather | solution.py:56
  36.3 24.8 %gather_fusion.1 = s32[6144]{0:T(1024)S(1)} fusion(s32[1024]{0:T(1024)S(1)} %add_subtract_fusion, s32[6144]{0:T(1024)S(1)} %broadcast_clamp_fusion), kind=kCustom, calls=%fused_computation.1 | custom fusion | bytes 73728 | tf_op jit(solution)/shard_map/gather | solution.py:57
  61.1 0.0 copy-start
  61.2 93.2 %fusion = f32[2048,512]{1,0:T(8,128)} fusion(f32[6144,512]{1,0:T(8,128)} %bitcast.18, f32[6144]{0:T(1024)S(1)} %get-tuple-element.11, s32[6144]{0:T(1024)S(1)} %gather_fusion.1, f32[6144]{0:T(1024)S(1)} %get-tuple-element.10, s32[6144]{0:T(1024)S(1)} %gather_fusion), kind=kOutput, calls=%fused_computation.2 | convolution fusion | flops 77372325888 | bytes 16875520 | tf_op jit(solution)/shard_map/dot_general | solution.py:69
  154.3 0.0 reduce-scatter.2.cloned.1.call-update
  154.4 0.0 all-gather.2.cloned.1.call-start
  154.4 0.2 select_reduce_fusion
  154.7 90.8 %reduce-scatter.2.cloned.1.call-done = f32[256,512]{1,0:T(8,128)} async-done(((f32[2048,512]{1,0:T(8,128)}), f32[256,512]{1,0:T(8,128)}) %reduce-scatter.2.cloned.1.call-update) | async-done | bytes 524304 | tf_op jit(solution)/shard_map/reduce_scatter | solution.py:68
  245.5 0.0 copy-done
  245.5 1.1 pad_maximum_fusion.4
  246.6 0.1 collective-permute-start
  246.7 1.7 collective-permute-start.1
  248.4 5.1 collective-permute-done
  253.5 0.8 collective-permute-done.1
  254.3 1.5 pad_maximum_fusion.2
  255.8 0.1 slice_bitcast_fusion.1
  255.9 0.5 fusion.28
  256.4 1.3 fusion.34
  257.7 0.0 all-gather.2.cloned.1.call-update
  257.7 3.8 fusion.33
  261.6 1.3 collective-permute-start.2
  262.9 4.6 collective-permute-start.3
  267.6 110.0 %all-gather.2.cloned.1.call-done = f32[2048,512]{1,0:T(8,128)} async-done(((f32[256,512]{1,0:T(8,128)}), f32[2048,512]{1,0:T(8,128)}) %all-gather.2.cloned.1.call-update) | async-done | bytes 4194320 | tf_op jit(solution)/shard_map/all_gather | solution.py:84
  377.6 123.0 %fusion.23 = f32[6144,512]{1,0:T(8,128)} fusion(f32[2048,512]{1,0:T(8,128)} %all-gather.2.cloned.1.call-done, f32[6144]{0:T(1024)S(1)} %reshape.131, s32[6144]{0:T(1024)S(1)} %gather_fusion.1, f32[6144]{0:T(1024)S(1)} %get-tuple-element.12, s32[6144]{0:T(1024)S(1)} %gather_fusion), kind=kOutput, calls=%fused_computation.31 | convolution fusion | flops 77375471616 | bytes 16875520 | tf_op jit(solution)/shard_map/dot_general | solution.py:88
  500.6 0.0 collective-permute-done.2
  500.6 0.0 collective-permute-done.3
  500.6 30.5 %fusion.22 = f32[8,768,512]{2,1,0:T(8,128)} fusion(f32[8,768,512]{2,1,0:T(8,128)} %param.6, f32[8,768,512]{2,1,0:T(8,128)} %bitcast.19, f32[1,768,512]{2,1,0:T(8,128)S(1)} %collective-permute-done.3, f32[1,768,512]{2,1,0:T(8,128)S(1)} %collective-permute-done.2, f32[768]{0:T(1024)S(1)} %get-tuple-element.17, f32[768]{0:T(1024)S(1)} %get-tuple-element.18), kind=kLoop, calls=%fused_computation.29 | loop fusion | flops 28311552 | bytes 40900608 | tf_op jit(solution)/shard_map/sub | solution.py:99
  (7 shorter events, 0.1 us)
Async XLA Ops:
  7.2 238.4 %reduce-scatter.2.cloned.1.call-start = ((), (), s32[]{:S(2)}) async-start(), calls=%async_computation.1 | async-start | bytes 4718592 | tf_op jit(solution)/shard_map/reduce_scatter | solution.py:68
  61.1 184.4 %copy-start = (f32[256,512]{1,0:T(8,128)S(1)}, f32[256,512]{1,0:T(8,128)}, u32[]{:S(2)}) copy-start(f32[256,512]{1,0:T(8,128)} %param.11) | copy-start | bytes 1572868
  154.4 223.2 %all-gather.2.cloned.1.call-start = ((), (), s32[]{:S(2)}) async-start(), calls=%async_computation.2 | async-start | bytes 4718592 | tf_op jit(solution)/shard_map/all_gather | solution.py:84
  246.6 6.9 %collective-permute-start = (f32[2,256,2]{2,1,0:T(8,128)S(1)}, f32[2,256,2]{2,1,0:T(8,128)S(1)}, u32[]{:S(2)}, u32[]{:S(2)}) collective-permute-start(f32[2,256,2]{2,1,0:T(8,128)S(1)} %get-tuple-element.6), channel_id=1, source_target_pairs={{0,1},{1,2},{2,3},{3,0},{4,5},{5,6},{6,7},{7,4},{8,9},{9,10},{10,1... | collective-permute-start | bytes 12296 | tf_op jit(solution)/shard_map/ppermute | solution.py:19
  246.7 7.6 %collective-permute-start.1 = (f32[2,256,2]{2,1,0:T(8,128)S(1)}, f32[2,256,2]{2,1,0:T(8,128)S(1)}, u32[]{:S(2)}, u32[]{:S(2)}) collective-permute-start(f32[2,256,2]{2,1,0:T(8,128)S(1)} %get-tuple-element.7), channel_id=1, source_target_pairs={{1,0},{2,1},{3,2},{0,3},{5,4},{6,5},{7,6},{4,7},{9,8},{10,9},{11,1... | collective-permute-start | bytes 12296 | tf_op jit(solution)/shard_map/ppermute | solution.py:20
  261.6 239.0 %collective-permute-start.2 = (f32[1,768,512]{2,1,0:T(8,128)}, f32[1,768,512]{2,1,0:T(8,128)S(1)}, u32[]{:S(2)}, u32[]{:S(2)}) collective-permute-start(f32[1,768,512]{2,1,0:T(8,128)} %get-tuple-element.2), channel_id=1, source_target_pairs={{4,0},{8,4},{12,8},{16,12},{20,16},{24,20},{28,24},{5,1},{9,5},{13... | collective-permute-start | bytes 4718600 | tf_op jit(solution)/shard_map/ppermute | solution.py:20
  262.9 237.7 %collective-permute-start.3 = (f32[1,768,512]{2,1,0:T(8,128)}, f32[1,768,512]{2,1,0:T(8,128)S(1)}, u32[]{:S(2)}, u32[]{:S(2)}) collective-permute-start(f32[1,768,512]{2,1,0:T(8,128)} %get-tuple-element.3), channel_id=1, source_target_pairs={{0,4},{4,8},{8,12},{12,16},{16,20},{20,24},{24,28},{1,5},{5,9},{9,... | collective-permute-start | bytes 4718600 | tf_op jit(solution)/shard_map/ppermute | solution.py:19
Sparse Core Ops, SparseCore 0:
  154.5 90.9 reduce-scatter.1
  257.9 119.6 all-gather.1
where the time goes:
time: 538 us
  matrix products  216 us (40%)
  waiting for transfers between devices  207 us (38%)
  local copies, waits for them, and re-layouts  55.7 us (10%)
  other arithmetic  37.3 us (7%)
  between operations  14.2 us (3%)
  starting transfers between devices  7.8 us (1%)
    dot_general x1, matrix products, per_device(): jnp.dot(interp, piece, precision=lax.Precision.HIGHEST, preferred_element...  123 us
    all_gather x1, waiting for transfers between devices, per_device(): piece = lax.all_gather(velocity, 'row', axis=0, tiled=True)  110 us
    dot_general x1, matrix products, per_device(): jnp.dot(banded, heat_vector_linear, precision=lax.Precision.HIGHEST, pref...  93.2 us
    reduce_scatter x1, waiting for transfers between devices, per_device(): lax.psum_scatter(jnp.dot(banded, heat_vector_linear, precision=lax.Precis...  90.8 us
    sub x1, other arithmetic, per_device(): thermal_state - thermal_advance * sphere_node_drift * (sin_theta_term * d...  30.5 us
    gather x1, local copies, waits for them, and re-layouts, per_device(): slot_low = slot_of_cell[lower_cell]  24.8 us
    gather x1, local copies, waits for them, and re-layouts, per_device(): slot_high = slot_of_cell[lower_cell + 1]  24.8 us
  transfers between devices with their start and end apart: 6, of which 4 were waited for; matrix products, arithmetic and copies ran while one was open for 24% of the time, Pallas kernels for 0%

commit v1 on v0

v1 whole, which is shorter than its diff:
```python
import functools
import math

import jax
import jax.numpy as jnp
from jax import lax
from jax.experimental import pallas as pl
from jax.experimental.pallas import tpu as pltpu
from jax.sharding import PartitionSpec as P

stream_step = 0.5
thermal_advance = 0.25
WINDOW = 256
STRIP = 32
LANES = 128


def split(x):
    high = x.astype(jnp.bfloat16)
    return high, (x - high.astype(jnp.float32)).astype(jnp.bfloat16)


def dot3(a_high, a_low, b_high, b_low):
    dot = functools.partial(jnp.dot, preferred_element_type=jnp.float32)
    return dot(a_high, b_high) + (dot(a_high, b_low) + dot(a_low, b_high))


def as_column(row):
    return jnp.broadcast_to(row, (LANES, row.shape[1])).T


def azimuth_difference(x, before, after, lanes):
    width = x.shape[1]
    left = jnp.where(lanes == 0, before, pltpu.roll(x, 1, 1))
    right = jnp.where(lanes == width - 1, after, pltpu.roll(x, width - 1, 1))
    return right - left


def geo_of(first, rows, cells):
    c = lax.broadcasted_iota(jnp.int32, (rows, 1), 0) + first
    return 1.0 / (0.25 + (c.astype(jnp.float32) + 0.5) / cells)


def integral_kernel(start, wins, t_ref, a_ref, f_ref, q_ref, z_ref, first_ref, last_ref, acc):
    i = pl.program_id(0)
    cells, width = z_ref.shape

    @pl.when(i == 0)
    def _():
        acc[...] = jnp.zeros_like(acc)

    t_high, t_low = split(t_ref[...].reshape(-1, width))
    a, f, q = a_ref[0], f_ref[0], q_ref[0]
    b_high, b_low = split(q * (1.0 - f))
    c_high, c_low = split(q * f)
    b_high, b_low, c_high, c_low = (x.astype(jnp.float32) for x in (b_high, b_low, c_high, c_low))
    row = lax.broadcasted_iota(jnp.int32, (WINDOW, a.shape[1]), 0)

    def window(k, carry):
        s = pl.multiple_of(start[i] + k * WINDOW, 16)
        d = row - (a - s)
        low, high = d == 0, d == 1
        w_high = jnp.where(low, b_high, jnp.where(high, c_high, 0.0)).astype(jnp.bfloat16)
        w_low = jnp.where(low, b_low, jnp.where(high, c_low, 0.0)).astype(jnp.bfloat16)
        acc[pl.ds(s, WINDOW), :] += dot3(w_high, w_low, t_high, t_low)
        return carry

    lax.fori_loop(0, wins[i], window, 0)

    @pl.when(i == pl.num_programs(0) - 1)
    def _():
        z_ref[...] = acc[0:cells, :]
        first_ref[...] = acc[0:cells, 0:LANES].T[0:8]
        last_ref[...] = acc[0:cells, width - LANES:width].T[LANES - 8:LANES]


def stream_kernel(own, z_ref, hb_ref, ha_ref, pot_ref, u_ref, pad):
    cells, width = z_ref.shape
    slots = pot_ref.shape[0]
    before, count = own[0], own[1]
    pad[cells:cells + slots, :] = pot_ref[...]
    lanes = lax.broadcasted_iota(jnp.int32, (LANES, width), 1)
    for c0 in range(0, cells, LANES):
        hb = as_column(hb_ref[7:8, c0:c0 + LANES])[:, 0:1]
        ha = as_column(ha_ref[0:1, c0:c0 + LANES])[:, 0:1]
        rows = slice(c0, c0 + LANES)
        diff = azimuth_difference(z_ref[rows, :], hb, ha, lanes)
        forcing = -geo_of(c0, LANES, cells) * (diff * 0.5)
        at = lax.broadcasted_iota(jnp.int32, (LANES, width), 0) + (c0 - before)
        from_row = cells + c0 - before
        tile = pl.multiple_of(from_row // 8 * 8, 8)
        held = pltpu.roll(pad[pl.ds(tile, LANES + 8), :], lax.rem(LANES + 8 - (from_row - tile), LANES + 8), 0)[:LANES]
        u_ref[rows, :] = stream_step * forcing + jnp.where((at >= 0) & (at < count), held, 0.0)


def advance_kernel(start, wins, g_ref, hb_ref, ha_ref, a_ref, f_ref, t_ref, up_ref, dn_ref,
                   in_ref, out_ref, sin_ref, cos_ref, o_ref, v_high, v_low, drift):
    i = pl.program_id(0)
    n = pl.num_programs(0)
    cells, width = g_ref.shape
    radii, strip, _ = t_ref.shape

    @pl.when(i == 0)
    def _():
        lanes = lax.broadcasted_iota(jnp.int32, (LANES, width), 1)
        for c0 in range(0, cells, LANES):
            rows = slice(c0, c0 + LANES)
            hb = as_column(hb_ref[7:8, rows])[:, 0:1]
            ha = as_column(ha_ref[0:1, rows])[:, 0:1]
            diff = azimuth_difference(g_ref[rows, :], hb, ha, lanes)
            high, low = split(geo_of(c0, LANES, cells) * (diff * 0.5))
            v_high[rows, :] = high
            v_low[rows, :] = low
        v_high[cells:, :] = jnp.zeros((v_high.shape[0] - cells, width), jnp.bfloat16)
        v_low[cells:, :] = jnp.zeros((v_low.shape[0] - cells, width), jnp.bfloat16)

    a = as_column(a_ref[0])
    f = as_column(f_ref[0])
    b_high, b_low = (x.astype(jnp.float32) for x in split(1.0 - f))
    c_high, c_low = (x.astype(jnp.float32) for x in split(f))
    lane = lax.broadcasted_iota(jnp.int32, a.shape, 1).astype(jnp.float32) - a
    drift[...] = jnp.zeros_like(drift)

    def window(k, carry):
        s = pl.multiple_of(start[i] + k * WINDOW, 16)
        highs, lows = [], []
        for h in range(0, WINDOW, LANES):
            d = lane + (s + h).astype(jnp.float32)
            low, high = d == 0.0, d == 1.0
            highs.append(jnp.where(low, b_high, jnp.where(high, c_high, 0.0)).astype(jnp.bfloat16))
            lows.append(jnp.where(low, b_low, jnp.where(high, c_low, 0.0)).astype(jnp.bfloat16))
        here = pl.ds(s, WINDOW)
        drift[...] += dot3(
            jnp.concatenate(highs, 1), jnp.concatenate(lows, 1), v_high[here, :], v_low[here, :]
        )
        return carry

    lax.fori_loop(0, wins[i], window, 0)

    tt = lax.broadcasted_iota(jnp.int32, (strip, width), 0)
    sine, cosine = sin_ref[...] * 0.5, cos_ref[...] * 0.5
    north_there = (i > 0).astype(jnp.float32)
    south_there = (i < n - 1).astype(jnp.float32)
    for r in range(radii):
        t = t_ref[r]
        inner = t_ref[r - 1] if r > 0 else in_ref[0]
        outer = t_ref[r + 1] if r < radii - 1 else out_ref[0]
        north = jnp.where(tt == 0, up_ref[r, 7:8, :] * north_there, pltpu.roll(t, 1, 0))
        south = jnp.where(tt == strip - 1, dn_ref[r, 0:1, :] * south_there, pltpu.roll(t, strip - 1, 0))
        slope = sine * (outer - inner) + cosine * (south - north)
        o_ref[r] = t - thermal_advance * drift[r * strip:(r + 1) * strip, :] * slope


def per_device(thermal, annulus, offset, share, holder, pot):
    radii, meridian, width = thermal.shape
    slots, cells = pot.shape[0], holder.shape[0]
    row = lax.axis_index("row")
    n_row, n_ma = lax.axis_size("row"), lax.axis_size("ma")
    count = meridian // STRIP
    points = radii * STRIP

    row_up = [(i, i + 1) for i in range(n_row - 1)]
    inner = lax.ppermute(thermal[-1:], "row", row_up)
    outer = lax.ppermute(thermal[:1], "row", [(j, i) for i, j in row_up])

    def arrange(x):
        return x.reshape(radii, count, STRIP).transpose(1, 0, 2).reshape(count, 1, points)

    a = arrange(annulus)
    f = arrange(offset)
    q = arrange(share)
    start = jnp.min(a, axis=(1, 2)) // 16 * 16
    wins = (jnp.max(a, axis=(1, 2)) + 1 - start) // WINDOW + 1
    own = jnp.stack([jnp.sum((holder < row).astype(jnp.int32)),
                     jnp.sum((holder == row).astype(jnp.int32))])

    small = pl.BlockSpec((1, 1, points), lambda i, *_: (i, 0, 0))
    slab = pl.BlockSpec((radii, STRIP, width), lambda i, *_: (0, i, 0))
    whole = lambda *shape: pl.BlockSpec(shape, lambda i, *_: (0,) * len(shape))
    f32 = lambda *shape: jax.ShapeDtypeStruct(shape, jnp.float32)
    flops = 6 * meridian * radii * WINDOW * width
    size = 4 * radii * meridian * width

    zint, first, last = pl.pallas_call(
        integral_kernel,
        grid_spec=pltpu.PrefetchScalarGridSpec(
            num_scalar_prefetch=2,
            grid=(count,),
            in_specs=[slab, small, small, small],
            out_specs=[whole(cells, width), whole(8, cells), whole(8, cells)],
            scratch_shapes=[pltpu.VMEM((cells + WINDOW, width), jnp.float32)],
        ),
        out_shape=[f32(cells, width), f32(8, cells), f32(8, cells)],
        cost_estimate=pl.CostEstimate(flops=flops, bytes_accessed=size, transcendentals=0),
        name="integral",
    )(start, wins, thermal, a, f, q)

    ma_up = [(i, (i + 1) % n_ma) for i in range(n_ma)]
    ma_down = [(j, i) for i, j in ma_up]
    stream = pl.pallas_call(
        stream_kernel,
        in_specs=[pl.BlockSpec(memory_space=pltpu.SMEM)] + [pl.BlockSpec(memory_space=pltpu.VMEM)] * 4,
        out_specs=pl.BlockSpec(memory_space=pltpu.VMEM),
        scratch_shapes=[pltpu.VMEM((2 * cells + LANES, width), jnp.float32)],
        out_shape=f32(cells, width),
        cost_estimate=pl.CostEstimate(flops=8 * cells * width, bytes_accessed=16 * cells * width, transcendentals=0),
        name="stream",
    )(own, zint, lax.ppermute(last, "ma", ma_up), lax.ppermute(first, "ma", ma_down), pot)

    stream = lax.psum_scatter(stream, "row", scatter_dimension=0, tiled=True)
    stream = lax.all_gather(stream, "row", axis=0, tiled=True)

    mine = lax.dynamic_slice(jnp.pad(stream, ((0, slots), (0, 0))), (own[0], 0), (slots, width))
    pot_later = jnp.where(jnp.arange(slots)[:, None] < own[1], mine, pot)
    first = jnp.broadcast_to(stream[:, 0][None, :], (8, cells))
    last = jnp.broadcast_to(stream[:, -1][None, :], (8, cells))
    angle = math.pi * (jnp.arange(meridian, dtype=jnp.float32) + 0.5) / meridian

    step = STRIP // 8
    ends = meridian // 8 - 1
    thermal_later = pl.pallas_call(
        advance_kernel,
        grid_spec=pltpu.PrefetchScalarGridSpec(
            num_scalar_prefetch=2,
            grid=(count,),
            in_specs=[
                whole(cells, width), whole(8, cells), whole(8, cells), small, small, slab,
                pl.BlockSpec((radii, 8, width), lambda i, *_: (0, jnp.maximum(i * step - 1, 0), 0)),
                pl.BlockSpec((radii, 8, width), lambda i, *_: (0, jnp.minimum(i * step + step, ends), 0)),
                pl.BlockSpec((1, STRIP, width), lambda i, *_: (0, i, 0)),
                pl.BlockSpec((1, STRIP, width), lambda i, *_: (0, i, 0)),
                pl.BlockSpec((STRIP, 1), lambda i, *_: (i, 0)),
                pl.BlockSpec((STRIP, 1), lambda i, *_: (i, 0)),
            ],
            out_specs=slab,
            scratch_shapes=[
                pltpu.VMEM((cells + WINDOW, width), jnp.bfloat16),
                pltpu.VMEM((cells + WINDOW, width), jnp.bfloat16),
                pltpu.VMEM((points, width), jnp.float32),
            ],
        ),
        out_shape=f32(radii, meridian, width),
        cost_estimate=pl.CostEstimate(flops=flops, bytes_accessed=2 * size, transcendentals=0),
        name="advance",
    )(start, wins, stream, lax.ppermute(last, "ma", ma_up), lax.ppermute(first, "ma", ma_down),
      a.astype(jnp.float32), f, thermal, thermal, thermal, inner, outer,
      jnp.sin(angle)[:, None], jnp.cos(angle)[:, None])
    return thermal_later, pot_later


def solution(mesh):
    return jax.shard_map(
        per_device,
        mesh=mesh,
        in_specs=(
            P("row", None, "ma"),
            P("row", None),
            P("row", None),
            P("row", None),
            P(),
            P("row", "ma"),
        ),
        out_specs=(P("row", None, "ma"), P("row", "ma")),
        check_vma=False,
    )
```

time: 538 us -> 261 us (0.49)
  matrix products: 216 us -> 0 us
  Pallas kernels: 0 us -> 59.3 us
  waiting for transfers between devices: 207 us -> 154 us
  local copies, waits for them, and re-layouts: 55.7 us -> 12.2 us
  other arithmetic: 37.3 us -> 9.51 us
    dot_general x2 -> x0, matrix products: 216 us -> none  [the longest x1 123 us: per_device(): jnp.dot(interp, piece, precision=lax.Precision.HIGHEST, preferred_element...]
    pallas_call x0 -> x3, Pallas kernels: none -> 59.3 us  [the longest x1 31.5 us: per_device(): pl.pallas_call(advance_kernel, grid_spec=pltpu.PrefetchScalarGridSpec(num...]
    gather x2 -> x0, local copies, waits for them, and re-layouts: 49.6 us -> none  [the longest x1 24.8 us: per_device(): slot_low = slot_of_cell[lower_cell]]
    sub x2 -> x0, other arithmetic: 31.2 us -> none  [the longest x1 30.5 us: per_device(): thermal_state - thermal_advance * sphere_node_drift * (sin_theta_term * d...]
    all_gather x1, waiting for transfers between devices: 110 us -> 83.1 us  [per_device(): stream = lax.all_gather(stream, 'row', axis=0, tiled=True)]
    reduce_scatter x1, waiting for transfers between devices: 90.8 us -> 70.7 us  [per_device(): stream = lax.psum_scatter(stream, 'row', scatter_dimension=0, tiled=True)]
    ppermute x4 -> x6, waiting for transfers between devices: 5.86 us -> 0.02 us  [the longest x2 0.01 us: per_device(): lax.ppermute(last, 'ma', ma_up)]
  transfers between devices with their start and end apart: 6 -> 8, of which waited for: 4 -> 2; matrix products, arithmetic and copies ran while one was open for 24% -> 5% of each run, Pallas kernels for 0% -> 0%
where the time goes in v1:
time: 261 us; the launch traced here: 259 us
  waiting for transfers between devices  154 us (59%)
  Pallas kernels  59.3 us (23%)
  between operations  15.9 us (6%)
  local copies, waits for them, and re-layouts  12.2 us (5%)
  other arithmetic  9.51 us (4%)
  starting transfers between devices  8.31 us (3%)
    all_gather x1, waiting for transfers between devices, per_device(): stream = lax.all_gather(stream, 'row', axis=0, tiled=True)  83.1 us
    reduce_scatter x1, waiting for transfers between devices, per_device(): stream = lax.psum_scatter(stream, 'row', scatter_dimension=0, tiled=True)  70.7 us
    pallas_call x1, Pallas kernels, per_device(): pl.pallas_call(advance_kernel, grid_spec=pltpu.PrefetchScalarGridSpec(num...  31.5 us
    pallas_call x1, Pallas kernels, per_device(): pl.pallas_call(integral_kernel, grid_spec=pltpu.PrefetchScalarGridSpec(nu...  22.5 us
    pallas_call x1, Pallas kernels, per_device(): pl.pallas_call(stream_kernel, in_specs=[pl.BlockSpec(memory_space=pltpu.S...  5.32 us
  transfers between devices with their start and end apart: 8, of which 2 were waited for; matrix products, arithmetic and copies ran while one was open for 5% of the time, Pallas kernels for 0%

profile of v1, /device:TPU:0, one launch (start us, length us, event | category | flops | bytes accessed | tf_op | source)
XLA Modules:
  0.0 259.1 jit_solution(1987867534997501866)
XLA Ops:
  7.2 0.0 reduce-scatter.2.cloned.1.call-start
  7.2 0.8 fusion.5
  8.0 0.8 reshape.60
  8.8 0.1 reduce_max.14
  8.9 0.1 reduce_min.14
  9.0 0.7 reshape.61.a_ref
  9.7 0.8 reshape.62
  10.5 0.7 reshape.63.f_ref
  11.3 0.8 reshape.64
  12.1 0.7 reshape.65.q_ref
  12.8 0.1 reduce_max.18
  13.0 0.1 reduce_min.18
  13.1 0.6 fusion.3
  13.7 22.5 %integral.1 = (f32[1024,512]{1,0:T(8,128)}, f32[8,1024]{1,0:T(8,128)}, f32[8,1024]{1,0:T(8,128)}) custom-call(s32[24]{0:T(128)} %get-tuple-element.15.start, s32[24]{0:T(128)} %get-tuple-element.14.wins, f32[8,768,512]{2,1,0:T(8,128)} %dn_ref.1, s32[24,1,256]{2,1,0:T(1,128)} %reshape.61.a_ref, f32[24,1,256]{2,1,0:T(1,128)} %reshape.63.f_ref, ...), custom_call_target="tpu_custom_call" | custom-call | flops 4831838208 | bytes 12582912 | tf_op jit(solution)/shard_map/integral/pallas_call | solution.py:184
  36.2 0.5 collective-permute-start
  36.7 2.0 collective-permute-start.1
  38.6 0.0 copy-done.7
  38.6 0.7 convert_reduce_fusion.1
  39.3 1.8 pad_add_fusion.own
  41.1 0.0 collective-permute-done.hb_ref
  41.1 0.0 collective-permute-done.1.ha_ref
  41.1 0.0 copy-start.6
  41.1 0.6 copy-done.5
  41.7 0.0 copy-done.6
  41.7 5.3 %stream.1 = f32[1024,512]{1,0:T(8,128)} custom-call(s32[2]{0:T(128)} %pad_add_fusion.own, f32[1024,512]{1,0:T(8,128)} %get-tuple-element.5.z_ref, f32[8,1024]{1,0:T(8,128)} %copy-done.5, f32[8,1024]{1,0:T(8,128)} %copy-done.6, f32[256,512]{1,0:T(8,128)} %pot_ref.1), custom_call_target="tpu_custom_call" | custom-call | flops 4194304 | bytes 8388608 | tf_op jit(solution)/shard_map/stream/pallas_call | solution.py:200
  47.0 0.0 reduce-scatter.2.cloned.1.call-update
  47.0 0.0 all-gather.2.cloned.1.call-start
  47.1 70.7 %reduce-scatter.2.cloned.1.call-done = f32[128,512]{1,0:T(8,128)} async-done(((f32[1024,512]{1,0:T(8,128)}), f32[128,512]{1,0:T(8,128)}) %reduce-scatter.2.cloned.1.call-update) | async-done | bytes 262160 | tf_op jit(solution)/shard_map/reduce_scatter | solution.py:210
  117.7 0.0 all-gather.2.cloned.1.call-update
  117.8 3.9 %fusion.7 = (f32[1,768,512]{2,1,0:T(8,128)}, f32[1,768,512]{2,1,0:T(8,128)}) fusion(f32[8,768,512]{2,1,0:T(8,128)} %dn_ref.1), kind=kLoop, calls=%fused_computation.25 | loop fusion | bytes 6291456 | tf_op jit(solution)/shard_map/slice | solution.py:164
  121.7 2.7 %collective-permute-start.4 = (f32[1,768,512]{2,1,0:T(8,128)}, f32[1,768,512]{2,1,0:T(8,128)S(1)}, u32[]{:S(2)}, u32[]{:S(2)}) collective-permute-start(f32[1,768,512]{2,1,0:T(8,128)} %get-tuple-element.17), channel_id=1, source_target_pairs={{0,4},{4,8},{8,12},{12,16},{16,20},{20,24},{24,28},{1,5},{5,9},{9,... | collective-permute-start | bytes 4718600 | tf_op jit(solution)/shard_map/ppermute | solution.py:163
  124.4 1.3 collective-permute-start.5
  125.7 0.6 convert_element_type.13.a_ref
  128.0 0.6 iota_compare_fusion
  128.6 2.3 fusion.1
  130.9 83.1 %all-gather.2.cloned.1.call-done.g_ref = f32[1024,512]{1,0:T(8,128)} async-done(((f32[128,512]{1,0:T(8,128)}), f32[1024,512]{1,0:T(8,128)}) %all-gather.2.cloned.1.call-update) | async-done | bytes 2097168 | tf_op jit(solution)/shard_map/all_gather | solution.py:211
  214.0 1.7 slice_reduce_fusion
  215.8 0.1 collective-permute-start.2
  215.8 1.7 collective-permute-start.3
  217.6 0.0 copy-done
  217.6 2.0 fusion
  219.5 0.0 collective-permute-done.4.in_ref
  219.5 0.0 collective-permute-done.5.out_ref
  219.5 0.0 collective-permute-done.2.hb_ref
  219.5 0.0 collective-permute-done.3.ha_ref
  219.6 1.1 copy-done.1
  220.7 0.0 copy-done.3
  220.7 31.5 %advance.1 = f32[8,768,512]{2,1,0:T(8,128)} custom-call(s32[24]{0:T(128)} %get-tuple-element.15.start, s32[24]{0:T(128)} %get-tuple-element.14.wins, f32[1024,512]{1,0:T(8,128)} %all-gather.2.cloned.1.call-done.g_ref, f32[8,1024]{1,0:T(8,128)} %copy-done.3, f32[8,1024]{1,0:T(8,128)} %copy-done.4, f32[24,1,256]{2,1,0:T(1,128)} %convert_element_type.13.a_ref, ...), custom_call_target="tpu_custom_call" | custom-call | flops 4831838208 | bytes 25165824 | tf_op jit(solution)/shard_map/advance/pallas_call | solution.py:221
  (14 shorter events, 0.1 us)
Async XLA Ops:
  7.2 110.6 %reduce-scatter.2.cloned.1.call-start = ((), (), s32[]{:S(2)}) async-start(), calls=%async_computation.1 | async-start | bytes 2359296 | tf_op jit(solution)/shard_map/reduce_scatter | solution.py:210
  13.7 24.9 %copy-start.7 = (s32[1024]{0:T(1024)S(1)}, s32[1024]{0:T(1024)}, u32[]{:S(2)}) copy-start(s32[1024]{0:T(1024)} %param.10) | copy-start | bytes 12292
  36.2 4.9 %collective-permute-start = (f32[8,1024]{1,0:T(8,128)}, f32[8,1024]{1,0:T(8,128)S(1)}, u32[]{:S(2)}, u32[]{:S(2)}) collective-permute-start(f32[8,1024]{1,0:T(8,128)} %get-tuple-element.6), channel_id=1, source_target_pairs={{0,1},{1,2},{2,3},{3,0},{4,5},{5,6},{6,7},{7,4},{8,9},{9,10},{10,1... | collective-permute-start | bytes 98312 | tf_op jit(solution)/shard_map/ppermute | solution.py:208
  36.7 4.4 %collective-permute-start.1 = (f32[8,1024]{1,0:T(8,128)}, f32[8,1024]{1,0:T(8,128)S(1)}, u32[]{:S(2)}, u32[]{:S(2)}) collective-permute-start(f32[8,1024]{1,0:T(8,128)} %get-tuple-element.7), channel_id=1, source_target_pairs={{1,0},{2,1},{3,2},{0,3},{5,4},{6,5},{7,6},{4,7},{9,8},{10,9},{11,1... | collective-permute-start | bytes 98312 | tf_op jit(solution)/shard_map/ppermute | solution.py:208
  41.1 0.6 copy-start.5
  41.1 0.6 copy-start.6
  47.0 167.0 %all-gather.2.cloned.1.call-start = ((), (), s32[]{:S(2)}) async-start(), calls=%async_computation.2 | async-start | bytes 2359296 | tf_op jit(solution)/shard_map/all_gather | solution.py:211
  117.8 7.9 %copy-start.2 = (s32[24,1,256]{2,1,0:T(1,128)S(1)}, s32[24,1,256]{2,1,0:T(1,128)}, u32[]{:S(2)}) copy-start(s32[24,1,256]{2,1,0:T(1,128)} %reshape.61.a_ref) | copy-start | bytes 73732
  121.7 95.9 %copy-start = (f32[256,512]{1,0:T(8,128)S(1)}, f32[256,512]{1,0:T(8,128)}, u32[]{:S(2)}) copy-start(f32[256,512]{1,0:T(8,128)} %pot_ref.1) | copy-start | bytes 1572868
  121.7 97.9 %collective-permute-start.4 = (f32[1,768,512]{2,1,0:T(8,128)}, f32[1,768,512]{2,1,0:T(8,128)S(1)}, u32[]{:S(2)}, u32[]{:S(2)}) collective-permute-start(f32[1,768,512]{2,1,0:T(8,128)} %get-tuple-element.17), channel_id=1, source_target_pairs={{0,4},{4,8},{8,12},{12,16},{16,20},{20,24},{24,28},{1,5},{5,9},{9,... | collective-permute-start | bytes 4718600 | tf_op jit(solution)/shard_map/ppermute | solution.py:163
  124.4 95.2 %collective-permute-start.5 = (f32[1,768,512]{2,1,0:T(8,128)}, f32[1,768,512]{2,1,0:T(8,128)}, u32[]{:S(2)}, u32[]{:S(2)}) collective-permute-start(f32[1,768,512]{2,1,0:T(8,128)} %get-tuple-element.16), channel_id=1, source_target_pairs={{4,0},{8,4},{12,8},{16,12},{20,16},{24,20},{28,24},{5,1},{9,5},{13... | collective-permute-start | bytes 4718600 | tf_op jit(solution)/shard_map/ppermute | solution.py:164
  215.8 3.8 %collective-permute-start.2 = (f32[8,1024]{1,0:T(8,128)S(1)}, f32[8,1024]{1,0:T(8,128)S(1)}, u32[]{:S(2)}, u32[]{:S(2)}) collective-permute-start(f32[8,1024]{1,0:T(8,128)S(1)} %broadcast_in_dim.26), channel_id=1, source_target_pairs={{0,1},{1,2},{2,3},{3,0},{4,5},{5,6},{6,7},{7,4},{8,9},{9,10},{10,1... | collective-permute-start | bytes 98312 | tf_op jit(solution)/shard_map/ppermute | solution.py:245
  215.8 3.7 %collective-permute-start.3 = (f32[8,1024]{1,0:T(8,128)S(1)}, f32[8,1024]{1,0:T(8,128)S(1)}, u32[]{:S(2)}, u32[]{:S(2)}) collective-permute-start(f32[8,1024]{1,0:T(8,128)S(1)} %broadcast_in_dim.28), channel_id=1, source_target_pairs={{1,0},{2,1},{3,2},{0,3},{5,4},{6,5},{7,6},{4,7},{9,8},{10,9},{11,1... | collective-permute-start | bytes 98312 | tf_op jit(solution)/shard_map/ppermute | solution.py:245
  219.5 1.2 copy-start.1
  219.5 1.2 copy-start.3
  219.6 1.1 copy-start.4
Sparse Core Ops, SparseCore 0:
  47.2 70.5 reduce-scatter.1
  119.9 94.1 all-gather.1

commit v2 on v1

--- a/solution.py
+++ b/solution.py
@@ -151,6 +151,59 @@
         o_ref[r] = t - thermal_advance * drift[r * strip:(r + 1) * strip, :] * slope
 
 
+def ring_kernel(n, u_ref, g_ref, got, total, send, recv):
+    me = lax.axis_index("row")
+    level, side = lax.div(me, 2), lax.rem(me, 2)
+    place = level * (1 - side) + (n - 1 - level) * side
+
+    def row_of(p):
+        back = lax.div(p, n // 2)
+        return 2 * (p * (1 - back) + (n - 1 - p) * back) + back
+
+    partner = (row_of(lax.rem(place + 1, n)), row_of(lax.rem(place + n - 1, n)))
+    mesh_id = pl.DeviceIdType.MESH
+    barrier = pltpu.get_barrier_semaphore()
+    for p in partner:
+        pl.semaphore_signal(barrier, inc=1, device_id={"row": p}, device_id_type=mesh_id)
+    pl.semaphore_wait(barrier, 2)
+
+    part = u_ref.shape[0] // n
+    half = part // 2
+
+    def rows(steps, d):
+        k = lax.rem(place + (2 * n - steps if d == 0 else steps), n)
+        return pl.ds(pl.multiple_of(k * part + d * half, 8), half)
+
+    def copy(s, d):
+        if s == 0:
+            source, target = u_ref.at[rows(1, d)], got.at[d, 0]
+        elif s < n - 1:
+            source, target = got.at[d, s - 1], got.at[d, s]
+        else:
+            source = target = total.at[rows(s - (n - 1), d)]
+        return pltpu.make_async_remote_copy(
+            src_ref=source, dst_ref=target, send_sem=send.at[d, s], recv_sem=recv.at[d, s],
+            device_id={"row": partner[d]}, device_id_type=mesh_id,
+        )
+
+    copies = [[copy(s, d) for d in (0, 1)] for s in range(2 * (n - 1))]
+    for d in (0, 1):
+        copies[0][d].start()
+    for s in range(2 * (n - 1)):
+        for d in (0, 1):
+            copies[s][d].wait_recv()
+            if s < n - 2:
+                got[d, s] = got[d, s] + u_ref[rows(s + 2, d), :]
+            elif s == n - 2:
+                total[rows(0, d), :] = got[d, s] + u_ref[rows(0, d), :]
+            if s + 1 < 2 * (n - 1):
+                copies[s + 1][d].start()
+    for pair in copies:
+        for d in (0, 1):
+            pair[d].wait_send()
+    g_ref[...] = total[...]
+
+
 def per_device(thermal, annulus, offset, share, holder, pot):
     radii, meridian, width = thermal.shape
     slots, cells = pot.shape[0], holder.shape[0]
@@ -178,8 +231,6 @@
     slab = pl.BlockSpec((radii, STRIP, width), lambda i, *_: (0, i, 0))
     whole = lambda *shape: pl.BlockSpec(shape, lambda i, *_: (0,) * len(shape))
     f32 = lambda *shape: jax.ShapeDtypeStruct(shape, jnp.float32)
-    flops = 6 * meridian * radii * WINDOW * width
-    size = 4 * radii * meridian * width
 
     zint, first, last = pl.pallas_call(
         integral_kernel,
@@ -191,7 +242,6 @@
             scratch_shapes=[pltpu.VMEM((cells + WINDOW, width), jnp.float32)],
         ),
         out_shape=[f32(cells, width), f32(8, cells), f32(8, cells)],
-        cost_estimate=pl.CostEstimate(flops=flops, bytes_accessed=size, transcendentals=0),
         name="integral",
     )(start, wins, thermal, a, f, q)
 
@@ -203,12 +253,24 @@
         out_specs=pl.BlockSpec(memory_space=pltpu.VMEM),
         scratch_shapes=[pltpu.VMEM((2 * cells + LANES, width), jnp.float32)],
         out_shape=f32(cells, width),
-        cost_estimate=pl.CostEstimate(flops=8 * cells * width, bytes_accessed=16 * cells * width, transcendentals=0),
         name="stream",
     )(own, zint, lax.ppermute(last, "ma", ma_up), lax.ppermute(first, "ma", ma_down), pot)
 
-    stream = lax.psum_scatter(stream, "row", scatter_dimension=0, tiled=True)
-    stream = lax.all_gather(stream, "row", axis=0, tiled=True)
+    part = cells // n_row // 2
+    stream = pl.pallas_call(
+        functools.partial(ring_kernel, n_row),
+        in_specs=[pl.BlockSpec(memory_space=pltpu.VMEM)],
+        out_specs=pl.BlockSpec(memory_space=pltpu.VMEM),
+        scratch_shapes=[
+            pltpu.VMEM((2, n_row - 1, part, width), jnp.float32),
+            pltpu.VMEM((cells, width), jnp.float32),
+            pltpu.SemaphoreType.DMA((2, 2 * (n_row - 1))),
+            pltpu.SemaphoreType.DMA((2, 2 * (n_row - 1))),
+        ],
+        out_shape=f32(cells, width),
+        compiler_params=pltpu.CompilerParams(collective_id=0, has_side_effects=True),
+        name="ring",
+    )(stream)
 
     mine = lax.dynamic_slice(jnp.pad(stream, ((0, slots), (0, 0))), (own[0], 0), (slots, width))
     pot_later = jnp.where(jnp.arange(slots)[:, None] < own[1], mine, pot)
@@ -240,7 +302,6 @@
             ],
         ),
         out_shape=f32(radii, meridian, width),
-        cost_estimate=pl.CostEstimate(flops=flops, bytes_accessed=2 * size, transcendentals=0),
         name="advance",
     )(start, wins, stream, lax.ppermute(last, "ma", ma_up), lax.ppermute(first, "ma", ma_down),
       a.astype(jnp.float32), f, thermal, thermal, thermal, inner, outer,

time: 261 us -> 184 us (0.70)
  waiting for transfers between devices: 154 us -> 0.02 us
  Pallas kernels: 59.3 us -> 150 us
  between operations: 15.9 us -> 2.54 us
    pallas_call x0 -> x1, Pallas kernels: none -> 90.9 us  [per_device(): pl.pallas_call(functools.partial(ring_kernel, n_row), in_specs=[pl.BlockS...]
    all_gather x1 -> x0, waiting for transfers between devices: 83.1 us -> none  [per_device(): stream = lax.all_gather(stream, 'row', axis=0, tiled=True)]
    reduce_scatter x1 -> x0, waiting for transfers between devices: 70.7 us -> none  [per_device(): stream = lax.psum_scatter(stream, 'row', scatter_dimension=0, tiled=True)]
  transfers between devices with their start and end apart: 8 -> 6, of which waited for: 2 -> 0; matrix products, arithmetic and copies ran while one was open for 5% -> 7% of each run, Pallas kernels for 0% -> 65%
where the time goes in v2:
time: 184 us; the launch traced here: 181 us
  Pallas kernels  150 us (82%)
  local copies, waits for them, and re-layouts  10 us (5%)
  starting transfers between devices  9.8 us (5%)
  other arithmetic  8.7 us (5%)
  between operations  2.54 us (1%)
    pallas_call x1, Pallas kernels, per_device(): pl.pallas_call(functools.partial(ring_kernel, n_row), in_specs=[pl.BlockS...  90.9 us
    pallas_call x1, Pallas kernels, per_device(): pl.pallas_call(advance_kernel, grid_spec=pltpu.PrefetchScalarGridSpec(num...  31.5 us
    pallas_call x1, Pallas kernels, per_device(): pl.pallas_call(integral_kernel, grid_spec=pltpu.PrefetchScalarGridSpec(nu...  22.5 us
    pallas_call x1, Pallas kernels, per_device(): pl.pallas_call(stream_kernel, in_specs=[pl.BlockSpec(memory_space=pltpu.S...  5.27 us
    ppermute x1, starting transfers between devices, per_device(): inner = lax.ppermute(thermal[-1:], 'row', row_up)  4.99 us
    slice x1, local copies, waits for them, and re-layouts, per_device(): outer = lax.ppermute(thermal[:1], 'row', [(j, i) for i, j in row_up])  3.95 us
  transfers between devices with their start and end apart: 6, of which 0 were waited for; matrix products, arithmetic and copies ran while one was open for 7% of the time, Pallas kernels for 65%

profile of v2, /device:TPU:0, one launch (start us, length us, event | category | flops | bytes accessed | tf_op | source)
XLA Modules:
  0.0 181.3 jit_solution(7313514150495822465)
XLA Ops:
  0.6 0.0 copy-start.3
  0.6 0.0 copy-start.8
  0.7 0.0 copy-start.9
  0.7 3.9 %fusion.7 = (f32[1,768,512]{2,1,0:T(8,128)}, f32[1,768,512]{2,1,0:T(8,128)}) fusion(f32[8,768,512]{2,1,0:T(8,128)} %dn_ref.1), kind=kLoop, calls=%fused_computation.25 | loop fusion | bytes 6291456 | tf_op jit(solution)/shard_map/slice | solution.py:217
  4.6 5.0 %collective-permute-start.4 = (f32[1,768,512]{2,1,0:T(8,128)}, f32[1,768,512]{2,1,0:T(8,128)S(1)}, u32[]{:S(2)}, u32[]{:S(2)}) collective-permute-start(f32[1,768,512]{2,1,0:T(8,128)} %get-tuple-element.17), channel_id=1, source_target_pairs={{0,4},{4,8},{8,12},{12,16},{16,20},{20,24},{24,28},{1,5},{5,9},{9,... | collective-permute-start | bytes 4718600 | tf_op jit(solution)/shard_map/ppermute | solution.py:216
  9.6 1.3 collective-permute-start.5
  10.9 0.0 copy-done.3
  10.9 0.1 reshape.60
  11.0 0.1 reduce_max.14
  11.1 0.1 reduce_min.14
  11.2 0.7 reshape.61.a_ref
  11.9 0.0 copy-done.8
  11.9 0.1 reshape.62
  12.0 0.7 reshape.63.f_ref
  12.8 0.0 copy-done.9
  12.8 0.1 reshape.64
  12.9 0.7 reshape.65.q_ref
  13.6 0.1 reduce_max.18
  13.7 0.1 reduce_min.18
  13.8 0.6 fusion.3
  14.4 22.5 %integral.1 = (f32[1024,512]{1,0:T(8,128)}, f32[8,1024]{1,0:T(8,128)}, f32[8,1024]{1,0:T(8,128)}) custom-call(s32[24]{0:T(128)} %get-tuple-element.15.start, s32[24]{0:T(128)} %get-tuple-element.14.wins, f32[8,768,512]{2,1,0:T(8,128)} %dn_ref.1, s32[24,1,256]{2,1,0:T(1,128)} %reshape.61.a_ref, f32[24,1,256]{2,1,0:T(1,128)} %reshape.63.f_ref, ...), custom_call_target="tpu_custom_call" | custom-call | tf_op jit(solution)/shard_map/integral/pallas_call | solution.py:235
  36.9 0.0 collective-permute-start
  36.9 1.7 collective-permute-start.1
  38.6 0.6 convert_reduce_fusion.1
  39.3 0.6 iota_compare_fusion
  39.9 2.3 %fusion.1 = (f32[768,1]{1,0:T(8,128)}, f32[768,1]{1,0:T(8,128)}) fusion(), kind=kLoop, calls=%fused_computation.5 | loop fusion | flops 1536 | bytes 6144 | tf_op jit(solution)/shard_map/cos | solution.py:308
  42.1 1.8 pad_add_fusion.own
  43.9 0.6 convert_element_type.13.a_ref
  46.2 0.0 collective-permute-done.hb_ref
  46.3 0.0 collective-permute-done.1.ha_ref
  46.3 0.0 copy-start.5
  46.3 0.6 copy-done.4
  46.9 0.0 copy-done.5
  46.9 5.3 %stream.1.u_ref = f32[1024,512]{1,0:T(8,128)} custom-call(s32[2]{0:T(128)} %pad_add_fusion.own, f32[1024,512]{1,0:T(8,128)} %get-tuple-element.5.z_ref, f32[8,1024]{1,0:T(8,128)} %copy-done.4, f32[8,1024]{1,0:T(8,128)} %copy-done.5, f32[256,512]{1,0:T(8,128)} %pot_ref.1), custom_call_target="tpu_custom_call" | custom-call | tf_op jit(solution)/shard_map/stream/pallas_call | solution.py:250
  52.2 90.9 %ring.1.g_ref = f32[1024,512]{1,0:T(8,128)} custom-call(f32[1024,512]{1,0:T(8,128)} %stream.1.u_ref), custom_call_target="tpu_custom_call" | custom-call | tf_op jit(solution)/shard_map/ring/pallas_call | solution.py:260
  143.1 1.7 slice_reduce_fusion
  144.8 0.1 collective-permute-start.2
  144.9 1.7 collective-permute-start.3
  146.6 2.0 %fusion = f32[256,512]{1,0:T(8,128)} fusion(f32[256,512]{1,0:T(8,128)S(1)} %copy-done, s32[]{:T(128)S(6)} %select_n.17, f32[1024,512]{1,0:T(8,128)} %ring.1.g_ref, pred[256]{0:T(512)(128)(4,1)S(1)} %iota_compare_fusion), kind=kLoop, calls=%fused_computation.1 | loop fusion | flops 131072 | bytes 3145988 | tf_op jit(solution)/shard_map/jit(_where)/select_n | solution.py:276
  148.6 0.0 collective-permute-done.2.hb_ref
  148.6 0.0 collective-permute-done.3.ha_ref
  148.6 0.0 collective-permute-done.4.in_ref
  148.6 0.0 copy-start.1
  148.6 0.0 collective-permute-done.5.out_ref
  148.6 0.6 copy-done.6
  149.2 0.0 copy-done.7
  149.2 0.5 copy-done.1
  149.8 31.5 %advance.1 = f32[8,768,512]{2,1,0:T(8,128)} custom-call(s32[24]{0:T(128)} %get-tuple-element.15.start, s32[24]{0:T(128)} %get-tuple-element.14.wins, f32[1024,512]{1,0:T(8,128)} %ring.1.g_ref, f32[8,1024]{1,0:T(8,128)} %copy-done.6, f32[8,1024]{1,0:T(8,128)} %copy-done.7, f32[24,1,256]{2,1,0:T(1,128)} %convert_element_type.13.a_ref, ...), custom_call_target="tpu_custom_call" | custom-call | tf_op jit(solution)/shard_map/advance/pallas_call | solution.py:283
  (15 shorter events, 0.1 us)
Async XLA Ops:
  0.6 10.3 %copy-start.3 = (s32[8,768]{1,0:T(8,128)S(1)}, s32[8,768]{1,0:T(8,128)}, u32[]{:S(2)}) copy-start(s32[8,768]{1,0:T(8,128)} %param.7) | copy-start | bytes 73732
  0.6 11.3 %copy-start.8 = (f32[8,768]{1,0:T(8,128)S(1)}, f32[8,768]{1,0:T(8,128)}, u32[]{:S(2)}) copy-start(f32[8,768]{1,0:T(8,128)} %param.8) | copy-start | bytes 73732
  0.7 12.1 %copy-start.9 = (f32[8,768]{1,0:T(8,128)S(1)}, f32[8,768]{1,0:T(8,128)}, u32[]{:S(2)}) copy-start(f32[8,768]{1,0:T(8,128)} %param.9) | copy-start | bytes 73732
  4.6 144.0 %collective-permute-start.4 = (f32[1,768,512]{2,1,0:T(8,128)}, f32[1,768,512]{2,1,0:T(8,128)S(1)}, u32[]{:S(2)}, u32[]{:S(2)}) collective-permute-start(f32[1,768,512]{2,1,0:T(8,128)} %get-tuple-element.17), channel_id=1, source_target_pairs={{0,4},{4,8},{8,12},{12,16},{16,20},{20,24},{24,28},{1,5},{5,9},{9,... | collective-permute-start | bytes 4718600 | tf_op jit(solution)/shard_map/ppermute | solution.py:216
  9.6 139.0 %collective-permute-start.5 = (f32[1,768,512]{2,1,0:T(8,128)}, f32[1,768,512]{2,1,0:T(8,128)}, u32[]{:S(2)}, u32[]{:S(2)}) collective-permute-start(f32[1,768,512]{2,1,0:T(8,128)} %get-tuple-element.16), channel_id=1, source_target_pairs={{4,0},{8,4},{12,8},{16,12},{20,16},{24,20},{28,24},{5,1},{9,5},{13... | collective-permute-start | bytes 4718600 | tf_op jit(solution)/shard_map/ppermute | solution.py:217
  14.4 24.2 %copy-start.10 = (s32[1024]{0:T(1024)S(1)}, s32[1024]{0:T(1024)}, u32[]{:S(2)}) copy-start(s32[1024]{0:T(1024)} %param.10) | copy-start | bytes 12292
  14.4 29.5 %copy-start.2 = (s32[24,1,256]{2,1,0:T(1,128)S(1)}, s32[24,1,256]{2,1,0:T(1,128)}, u32[]{:S(2)}) copy-start(s32[24,1,256]{2,1,0:T(1,128)} %reshape.61.a_ref) | copy-start | bytes 73732
  36.9 9.4 %collective-permute-start = (f32[8,1024]{1,0:T(8,128)}, f32[8,1024]{1,0:T(8,128)S(1)}, u32[]{:S(2)}, u32[]{:S(2)}) collective-permute-start(f32[8,1024]{1,0:T(8,128)} %get-tuple-element.6), channel_id=1, source_target_pairs={{0,1},{1,2},{2,3},{3,0},{4,5},{5,6},{6,7},{7,4},{8,9},{9,10},{10,1... | collective-permute-start | bytes 98312 | tf_op jit(solution)/shard_map/ppermute | solution.py:257
  36.9 9.4 %collective-permute-start.1 = (f32[8,1024]{1,0:T(8,128)}, f32[8,1024]{1,0:T(8,128)S(1)}, u32[]{:S(2)}, u32[]{:S(2)}) collective-permute-start(f32[8,1024]{1,0:T(8,128)} %get-tuple-element.7), channel_id=1, source_target_pairs={{1,0},{2,1},{3,2},{0,3},{5,4},{6,5},{7,6},{4,7},{9,8},{10,9},{11,1... | collective-permute-start | bytes 98312 | tf_op jit(solution)/shard_map/ppermute | solution.py:257
  46.2 0.6 copy-start.4
  46.3 0.6 copy-start.5
  52.2 94.5 %copy-start = (f32[256,512]{1,0:T(8,128)S(1)}, f32[256,512]{1,0:T(8,128)}, u32[]{:S(2)}) copy-start(f32[256,512]{1,0:T(8,128)} %pot_ref.1) | copy-start | bytes 1572868
  144.8 3.8 %collective-permute-start.2 = (f32[8,1024]{1,0:T(8,128)S(1)}, f32[8,1024]{1,0:T(8,128)S(1)}, u32[]{:S(2)}, u32[]{:S(2)}) collective-permute-start(f32[8,1024]{1,0:T(8,128)S(1)} %broadcast_in_dim.26), channel_id=1, source_target_pairs={{0,1},{1,2},{2,3},{3,0},{4,5},{5,6},{6,7},{7,4},{8,9},{9,10},{10,1... | collective-permute-start | bytes 98312 | tf_op jit(solution)/shard_map/ppermute | solution.py:306
  144.9 3.7 %collective-permute-start.3 = (f32[8,1024]{1,0:T(8,128)S(1)}, f32[8,1024]{1,0:T(8,128)S(1)}, u32[]{:S(2)}, u32[]{:S(2)}) collective-permute-start(f32[8,1024]{1,0:T(8,128)S(1)} %broadcast_in_dim.28), channel_id=1, source_target_pairs={{1,0},{2,1},{3,2},{0,3},{5,4},{6,5},{7,6},{4,7},{9,8},{10,9},{11,1... | collective-permute-start | bytes 98312 | tf_op jit(solution)/shard_map/ppermute | solution.py:306
  148.6 0.6 copy-start.6
  148.6 0.6 copy-start.7
  148.6 1.1 copy-start.1
